TPU v7x, 32 devices: a 4x4x1 block of a 4x4x8 slice. The times are simulated.
32 devices in a mesh: dp: 1 (over z), x: 32 (over y, x, core).
Axes of the slice: x: 4, y: 4, z: 1, core: 2. Of those that a mesh axis runs over, the one named last changes fastest.
The devices are a block of a 4x4x8 slice.
Arguments:
- c_raw: bfloat16 [512, 1024, 512], P('dp', 'x')
- k_raw: bfloat16 [512, 1024, 64], P('dp', 'x')
- norm_gain: bfloat16 [512], replicated
- rope_cos: float32 [1024, 32], P('x')
- rope_sin: float32 [1024, 32], P('x')
- seq_lens: int32 [512], P('dp')
- q_lat: bfloat16 [512, 16, 512], P(('dp', 'x'))
- q_rope: bfloat16 [512, 16, 64], P(('dp', 'x'))
Outputs:
- output 1: bfloat16 [512, 1024, 512], P(('dp', 'x'))
- output 2: bfloat16 [512, 1024, 64], P(('dp', 'x'))
- output 3: bfloat16 [512, 16, 512], P(('dp', 'x'))
All inputs are finite; a program needn't handle non-finite values.
Results may differ from a plain program's by a relative error of at most 0.00590157.
Values are sent between devices in bfloat16 or wider.
A program may use at most 768 MiB of HBM per device.

v0:
```python
import jax
import jax.numpy as jnp
from jax import lax
from jax.sharding import PartitionSpec as P

NORM_EPS = 1e-6


def normed_rope(c_raw, k_raw, norm_gain, rope_cos, rope_sin, valid):
    lat_f32 = c_raw.astype(jnp.float32)
    inv_rms = lax.rsqrt(jnp.mean(lat_f32 * lat_f32, axis=-1, keepdims=True) + NORM_EPS)
    c_norm = jnp.where(valid[..., None], lat_f32 * inv_rms * norm_gain.astype(jnp.float32), 0.0)
    half_dim = k_raw.shape[-1] // 2
    key_f32 = k_raw.astype(jnp.float32)
    key_lo = key_f32[..., :half_dim]
    key_hi = key_f32[..., half_dim:]
    rotated = jnp.concatenate([key_lo * rope_cos - key_hi * rope_sin, key_hi * rope_cos + key_lo * rope_sin], axis=-1)
    k_rope = jnp.where(valid[..., None], rotated, 0.0)
    return c_norm.astype(jnp.bfloat16), k_rope.astype(jnp.bfloat16)


def latent_attention(q_lat, q_rope, c_cache, kr_cache, valid):
    attn_scale = (q_lat.shape[-1] + q_rope.shape[-1]) ** -0.5
    scores = jnp.einsum("rhk,rsk->rhs", q_lat, c_cache, preferred_element_type=jnp.float32)
    scores = scores + jnp.einsum("rhe,rse->rhs", q_rope, kr_cache, preferred_element_type=jnp.float32)
    scores = jnp.where(valid[:, None, :], scores * attn_scale, -1e30)
    weights = jnp.exp(scores - jnp.max(scores, axis=-1, keepdims=True))
    weight_sum = jnp.sum(weights, axis=-1)
    weighted = jnp.einsum("rhs,rsk->rhk", weights.astype(jnp.bfloat16), c_cache, preferred_element_type=jnp.float32)
    return (weighted / weight_sum[..., None]).astype(jnp.bfloat16)


def solution(mesh):
    seq_spec = P("dp", "x", None)
    req_spec = P(("dp", "x"), None, None)

    def local_step(c_raw, k_raw, norm_gain, rope_cos, rope_sin, seq_lens, q_lat, q_rope):
        dev_index = lax.axis_index("x")
        seq_local = c_raw.shape[1]
        req_local = q_lat.shape[0]
        positions = dev_index * seq_local + jnp.arange(seq_local)
        valid = positions[None, :] < seq_lens[:, None]
        c_norm, k_rope = normed_rope(c_raw, k_raw, norm_gain, rope_cos, rope_sin, valid)
        c_cache = lax.all_to_all(c_norm, "x", 0, 1, tiled=True)
        kr_cache = lax.all_to_all(k_rope, "x", 0, 1, tiled=True)
        own_lens = lax.dynamic_slice_in_dim(seq_lens, dev_index * req_local, req_local)
        own_valid = jnp.arange(c_cache.shape[1])[None, :] < own_lens[:, None]
        o_lat = latent_attention(q_lat, q_rope, c_cache, kr_cache, own_valid)
        return c_cache, kr_cache, o_lat

    return jax.shard_map(local_step, mesh=mesh, in_specs=(seq_spec, seq_spec, P(None), P("x", None), P("x", None), P("dp"), req_spec, req_spec), out_specs=(req_spec, req_spec, req_spec), check_vma=False)
```

profile of v0, /device:TPU:107, one launch (start us, length us, event | category | flops | bytes accessed | tf_op | source)
XLA Modules:
  0.0 317.4 jit_solution(17176617235911112784)
XLA Ops:
  0.6 0.0 copy-start
  0.7 0.0 copy-start.5
  0.7 0.0 copy-start.3
  0.7 0.0 copy-start.4
  0.7 7.4 %copy.15 = bf16[512,32,64]{2,1,0:T(8,128)(2,1)} copy(bf16[512,32,64]{0,2,1:T(8,128)(2,1)} %param.9) | data formatting | bytes 4194304 | tf_op args[1]
  8.1 3.4 %convert_element_type.24 = f32[512,32,64]{2,1,0:T(8,128)S(1)} convert(bf16[512,32,64]{2,1,0:T(8,128)(2,1)} %copy.15) | non-fusion elementwise | flops 1048576 | bytes 6291456 | tf_op jit(solution)/shard_map/convert_element_type | solution.py:14
  11.5 0.0 copy-done.5
  11.5 0.1 broadcast_compare_fusion
  11.7 0.0 copy-done.3
  11.7 0.0 copy-done.4
  11.7 2.8 multiply_subtract_fusion
  14.5 8.5 %fusion.4 = bf16[512,32,64]{2,1,0:T(8,128)(2,1)} fusion(bf16[512,32,32]{2,1,0:T(8,128)(2,1)S(1)} %get-tuple-element.7, bf16[512,32,32]{2,1,0:T(8,128)(2,1)S(1)} %get-tuple-element.6, pred[512,32]{1,0:T(8,128)(4,1)S(1)} %broadcast_compare_fusion), kind=kLoop, calls=%fused_computation.7 | loop fusion | flops 5242880 | bytes 4210688 | tf_op jit(solution)/shard_map/convert_element_type | solution.py:19
  22.9 0.0 copy-start.6
  22.9 7.9 %reshape.68 = bf16[32,2,16384]{2,1,0:T(2,128)(2,1)} reshape(bf16[512,32,64]{2,1,0:T(8,128)(2,1)} %fusion.4) | data formatting | bytes 4194304
  30.8 7.7 %all-to-all-start.1 = ((bf16[32,2,16384]{2,1,0:T(2,128)(2,1)}), bf16[32,2,16384]{2,1,0:T(2,128)(2,1)S(1)}, u32[]{:S(2)}, u32[]{:S(2)}) async-start(bf16[32,2,16384]{2,1,0:T(2,128)(2,1)} %reshape.68), calls=%async_computation.1 | async-start | bytes 4194304 | tf_op jit(solution)/shard_map/all_to_all | solution.py:45
  38.5 0.0 copy-done.6
  38.5 7.2 %fusion = f32[512,32]{1,0:T(8,128)S(1)} fusion(bf16[512,32,512]{2,1,0:T(8,128)(2,1)} %param.8), kind=kLoop, calls=%fused_computation.2 | loop fusion | flops 25149440 | bytes 16842752 | tf_op jit(solution)/shard_map/reduce_sum | solution.py:11
  45.8 14.4 %fusion.3 = bf16[512,32,512]{2,1,0:T(8,128)(2,1)} fusion(bf16[512,32,512]{2,1,0:T(8,128)(2,1)} %param.8, f32[512]{0:T(512)S(1)} %convert_element_type.22, f32[512,32]{1,0:T(8,128)S(1)} %add_rsqrt_fusion, pred[512,32]{1,0:T(8,128)(4,1)S(1)} %broadcast_compare_fusion), kind=kLoop, calls=%fused_computation.5 | loop fusion | flops 41943040 | bytes 33638400 | tf_op jit(solution)/shard_map/convert_element_type | solution.py:19
  60.2 5.5 %all-to-all-done.1 = bf16[32,2,16384]{2,1,0:T(2,128)(2,1)S(1)} async-done(((bf16[32,2,16384]{2,1,0:T(2,128)(2,1)}), bf16[32,2,16384]{2,1,0:T(2,128)(2,1)S(1)}, u32[]{:S(2)}, u32[]{:S(2)}) %all-to-all-start.1) | async-done | bytes 2097184 | tf_op jit(solution)/shard_map/all_to_all | solution.py:45
  65.7 7.0 %all-to-all-start = ((bf16[512,32,512]{2,1,0:T(8,128)(2,1)}), bf16[512,32,512]{2,1,0:T(8,128)(2,1)}, u32[]{:S(2)}, u32[]{:S(2)}) async-start(bf16[512,32,512]{2,1,0:T(8,128)(2,1)} %fusion.3), calls=%async_computation | async-start | bytes 33554432 | tf_op jit(solution)/shard_map/all_to_all | solution.py:44
  72.7 0.1 dynamic_slice.3
  72.8 0.1 iota_compare_fusion
  72.8 4.0 %reshape.69 = bf16[512,32,64]{2,1,0:T(8,128)(2,1)} reshape(bf16[32,2,16384]{2,1,0:T(2,128)(2,1)S(1)} %all-to-all-done.1) | data formatting | bytes 4194304
  76.8 5.2 %copy.16 = bf16[16,32,32,64]{3,2,1,0:T(8,128)(2,1)} copy(bf16[16,32,32,64]{3,2,0,1:T(8,128)(2,1)} %bitcast.20) | data formatting | bytes 4194304 | tf_op jit(solution)/shard_map/all_to_all | solution.py:45
  82.1 4.8 %copy.18 = bf16[16,1024,64]{1,2,0:T(8,128)(2,1)} copy(bf16[16,1024,64]{2,1,0:T(8,128)(2,1)} %bitcast.18) | data formatting | bytes 4194304
  86.8 209.6 %all-to-all-done = bf16[512,32,512]{2,1,0:T(8,128)(2,1)} async-done(((bf16[512,32,512]{2,1,0:T(8,128)(2,1)}), bf16[512,32,512]{2,1,0:T(8,128)(2,1)}, u32[]{:S(2)}, u32[]{:S(2)}) %all-to-all-start) | async-done | bytes 16777248 | tf_op jit(solution)/shard_map/all_to_all | solution.py:44
  296.4 8.4 %copy.14 = bf16[32,16,32,512]{3,2,0,1:T(8,128)(2,1)S(1)} copy(bf16[32,16,32,512]{3,2,1,0:T(8,128)(2,1)} %bitcast) | data formatting | bytes 33554432 | tf_op jit(solution)/shard_map/all_to_all | solution.py:44
  304.8 0.0 copy-start.1
  304.8 0.0 copy-done
  304.8 0.0 copy-start.2
  304.8 4.5 %fusion.14 = f32[16,1024,16]{1,2,0:T(8,128)S(1)} fusion(bf16[16,1024,512]{2,1,0:T(8,128)(2,1)S(1)} %bitcast.15, bf16[16,16,512]{2,1,0:T(8,128)(2,1)S(1)} %copy-done), kind=kOutput, calls=%fused_computation.25 | convolution fusion | flops 268435456 | bytes 18087936 | tf_op jit(solution)/shard_map/rhk,rsk->rhs/dot_general | solution.py:24
  309.3 0.0 copy-done.2
  309.3 4.7 %fusion.13 = (f32[16,16]{1,0:T(8,128)S(1)}, f32[16,16,1024]{2,1,0:T(8,128)S(1)}) fusion(f32[16,1024,16]{1,2,0:T(8,128)S(1)} %fusion.14, bf16[16,1024,64]{2,1,0:T(8,128)(2,1)} %bitcast.19, bf16[16,16,64]{2,1,0:T(8,128)(2,1)S(1)} %copy-done.2, pred[16,1024]{1,0:T(8,128)(4,1)S(1)} %iota_compare_fusion), kind=kOutput, calls=%fused_computation.24 | convolution fusion | flops 34602752 | bytes 4244480 | tf_op jit(solution)/shard_map/rhe,rse->rhs/dot_general | solution.py:25
  314.0 0.3 fusion.9
  314.3 0.0 copy-done.1
  314.3 3.0 fusion.8
  (3 shorter events, 0.1 us)
Async XLA Ops:
  0.6 304.2 %copy-start = (bf16[16,16,512]{2,1,0:T(8,128)(2,1)S(1)}, bf16[16,16,512]{2,1,0:T(8,128)(2,1)}, u32[]{:S(2)}) copy-start(bf16[16,16,512]{2,1,0:T(8,128)(2,1)} %param.14) | copy-start | bytes 786436
  0.7 10.9 %copy-start.5 = (s32[512]{0:T(512)S(1)}, s32[512]{0:T(512)}, u32[]{:S(2)}) copy-start(s32[512]{0:T(512)} %param.13) | copy-start | bytes 6148
  0.7 11.0 %copy-start.3 = (f32[32,32]{1,0:T(8,128)S(1)}, f32[32,32]{1,0:T(8,128)}, u32[]{:S(2)}) copy-start(f32[32,32]{1,0:T(8,128)} %param.12) | copy-start | bytes 12292
  0.7 11.0 %copy-start.4 = (f32[32,32]{1,0:T(8,128)S(1)}, f32[32,32]{1,0:T(8,128)}, u32[]{:S(2)}) copy-start(f32[32,32]{1,0:T(8,128)} %param.11) | copy-start | bytes 12292
  22.9 15.6 %copy-start.6 = (bf16[512]{0:T(512)(128)(2,1)S(1)}, bf16[512]{0:T(512)(128)(2,1)}, u32[]{:S(2)}) copy-start(bf16[512]{0:T(512)(128)(2,1)} %param.10) | copy-start | bytes 3076
  30.8 34.8 %all-to-all-start.1 = ((bf16[32,2,16384]{2,1,0:T(2,128)(2,1)}), bf16[32,2,16384]{2,1,0:T(2,128)(2,1)S(1)}, u32[]{:S(2)}, u32[]{:S(2)}) async-start(bf16[32,2,16384]{2,1,0:T(2,128)(2,1)} %reshape.68), calls=%async_computation.1 | async-start | bytes 4194304 | tf_op jit(solution)/shard_map/all_to_all | solution.py:45
  65.7 230.7 %all-to-all-start = ((bf16[512,32,512]{2,1,0:T(8,128)(2,1)}), bf16[512,32,512]{2,1,0:T(8,128)(2,1)}, u32[]{:S(2)}, u32[]{:S(2)}) async-start(bf16[512,32,512]{2,1,0:T(8,128)(2,1)} %fusion.3), calls=%async_computation | async-start | bytes 33554432 | tf_op jit(solution)/shard_map/all_to_all | solution.py:44
  304.8 9.5 %copy-start.1 = (bf16[32,16,32,512]{3,2,0,1:T(8,128)(2,1)}, bf16[32,16,32,512]{3,2,0,1:T(8,128)(2,1)S(1)}, u32[]{:S(2)}) copy-start(bf16[32,16,32,512]{3,2,0,1:T(8,128)(2,1)S(1)} %copy.14) | copy-start | bytes 50331652
  304.8 4.5 %copy-start.2 = (bf16[16,16,64]{2,1,0:T(8,128)(2,1)S(1)}, bf16[16,16,64]{2,1,0:T(8,128)(2,1)}, u32[]{:S(2)}) copy-start(bf16[16,16,64]{2,1,0:T(8,128)(2,1)} %param.15) | copy-start | bytes 98308
where the time goes:
time: 318 us; the launch traced here: 317 us
  waiting for transfers between devices  215 us (68%)
  local copies, waits for them, and re-layouts  37.8 us (12%)
  other arithmetic  36.8 us (12%)
  starting transfers between devices  14.7 us (5%)
  matrix products  12.2 us (4%)
    all_to_all x1, waiting for transfers between devices, local_step(): c_cache = lax.all_to_all(c_norm, 'x', 0, 1, tiled=True)  210 us
    unnamed x18, local copies, waits for them, and re-layouts  24.1 us
    convert_element_type x2, other arithmetic, normed_rope(): return (c_norm.astype(jnp.bfloat16), k_rope.astype(jnp.bfloat16))  22.9 us
    all_to_all x1, local copies, waits for them, and re-layouts, local_step(): c_cache = lax.all_to_all(c_norm, 'x', 0, 1, tiled=True)  8.41 us
    all_to_all x1, starting transfers between devices, local_step(): kr_cache = lax.all_to_all(k_rope, 'x', 0, 1, tiled=True)  7.66 us
    reduce_sum x1, other arithmetic, normed_rope(): jnp.mean(lat_f32 * lat_f32, axis=-1, keepdims=True) + NORM_EPS  7.2 us
    all_to_all x1, starting transfers between devices, local_step(): c_cache = lax.all_to_all(c_norm, 'x', 0, 1, tiled=True)  6.99 us
  transfers between devices with their start and end apart: 2, of which 2 were waited for; matrix products, arithmetic and copies ran while one was open for 11% of the time, Pallas kernels for 0%

commit v1 on v0

v1 whole, which is shorter than its diff:
```python
import jax
import jax.numpy as jnp
from jax import lax
from jax.experimental import pallas as pl
from jax.experimental.pallas import tpu as pltpu
from jax.sharding import PartitionSpec as P

NORM_EPS = 1e-6
MESH = pl.DeviceIdType.MESH
MIB = 2**20

OFFSETS = ((2, 2), (1, 1), (3, 3), (1, 3), (3, 1), (1, 2), (3, 0), (3, 2), (1, 0), (2, 1), (0, 3), (2, 3), (0, 1), (2, 0), (0, 2), (0, 0))
SIDE = 4
CORES = 2


def table(values, index):
    out = jnp.int32(values[0])
    for place, value in enumerate(values[1:], 1):
        out = jnp.where(index == place, jnp.int32(value), out)
    return out


def chip_at(me, dx, dy):
    chip = me // CORES
    return lax.rem(chip // SIDE + dy, SIDE) * SIDE + lax.rem(lax.rem(chip, SIDE) + dx, SIDE)


def exchange_kernel(lens_s, c_raw, k_raw, gain, cos, sin, lens_v, c_out, k_out, raw, send_c, k_in, k_rows, send_k, raw_sem, k_sem, c_send, c_recv, k_send, k_recv):
    me = lax.axis_index("x")
    group = lax.axis_index("dp")
    core = lax.rem(me, CORES)
    n_dev = SIDE * SIDE * CORES
    n_off = len(OFFSETS)
    seq_local = c_raw.shape[1]
    req_local = c_out.shape[0]
    half = cos.shape[1]
    first_pos = me * seq_local
    pair_req = CORES * req_local
    dxs = [o[0] for o in OFFSETS]
    dys = [o[1] for o in OFFSETS]

    barrier = pltpu.get_barrier_semaphore()

    def greet(step, carry):
        pl.semaphore_signal(barrier, inc=1, device_id=(group, lax.rem(me + step, n_dev)), device_id_type=MESH)
        return carry

    lax.fori_loop(1, n_dev, greet, 0)

    def chip_of(o):
        return chip_at(me, table(dxs, o), table(dys, o))

    def load(o, slot):
        return pltpu.make_async_copy(c_raw.at[pl.ds(chip_of(o) * pair_req, pair_req)], raw.at[slot], raw_sem.at[slot])

    def norm_one(o, chip, slot, row, store):
        length = lens_s[chip * pair_req + row]
        x = raw[slot, row].astype(jnp.float32)
        inv = lax.rsqrt(jnp.mean(x * x, axis=-1, keepdims=True) + NORM_EPS)
        valid = first_pos + lax.broadcasted_iota(jnp.int32, inv.shape, 0) < length
        y = x * inv * gain[...].astype(jnp.float32)
        store(jnp.where(valid, y, 0.0).astype(jnp.bfloat16))

    def c_copy(o, dc):
        chip = chip_of(o)
        there = lax.rem(core + dc, CORES)
        return pltpu.make_async_remote_copy(
            send_c.at[o, pl.ds(there * req_local, req_local)],
            c_out.at[:, pl.ds(pl.multiple_of(first_pos, 32), seq_local), :],
            c_send.at[o, dc],
            c_recv.at[o, dc],
            device_id=(group, chip * CORES + there),
            device_id_type=MESH,
        )

    def k_copy(o, dc):
        chip = chip_of(o)
        there = lax.rem(core + dc, CORES)
        dest = chip * CORES + there
        return pltpu.make_async_remote_copy(
            send_k.at[pl.ds(dest * req_local, req_local)],
            k_out.at[:, pl.ds(pl.multiple_of(me * (seq_local // 2), 16), seq_local // 2), :],
            k_send.at[o, dc],
            k_recv.at[o, dc],
            device_id=(group, dest),
            device_id_type=MESH,
        )

    def norm_chip(o, slot):
        chip = chip_of(o)

        def body(row, carry):
            def store(y):
                send_c[o, row] = y

            norm_one(o, chip, slot, row, store)
            return carry

        lax.fori_loop(0, pair_req, body, 0, unroll=4)

    k_load = pltpu.make_async_copy(k_raw, k_in, k_sem)
    load(0, 0).start()
    k_load.start()
    load(1, 1).start()
    load(0, 0).wait()
    norm_chip(0, 0)
    load(2, 0).start()

    k_load.wait()
    cos_t = cos[...].T
    sin_t = sin[...].T
    pairs = seq_local // 2
    lane_valid = lens_v[...]

    for pair in range(pairs):
        pieces = []
        for pos in (pair, pair + pairs):
            lo = k_in[pos, :half, :].astype(jnp.float32)
            hi = k_in[pos, half:, :].astype(jnp.float32)
            c = cos_t[:, pos : pos + 1]
            s = sin_t[:, pos : pos + 1]
            keep = first_pos + pos < lane_valid
            pieces.append(jnp.where(keep, lo * c - hi * s, 0.0))
            pieces.append(jnp.where(keep, hi * c + lo * s, 0.0))
        both = jnp.concatenate(pieces, axis=0)
        k_rows[pl.ds(pair, k_rows.shape[0] // pairs, stride=pairs), :] = both.T

    def pack(step, carry):
        rows = k_rows[pl.ds(pl.multiple_of(step * 256, 256), 256), :].astype(jnp.bfloat16)
        send_k[pl.ds(step * 16, 16)] = rows.reshape(16, 16, 128)
        return carry

    lax.fori_loop(0, n_dev, pack, 0)

    pl.semaphore_wait(barrier, n_dev - 1)
    c_copy(0, 0).start()
    c_copy(0, 1).start()

    def start_k(o, carry):
        k_copy(o, 0).start()
        k_copy(o, 1).start()
        return carry

    lax.fori_loop(0, n_off - 1, start_k, 0)
    k_copy(n_off - 1, 1).start()
    k_out[:, pl.ds(pl.multiple_of(me * pairs, 16), pairs), :] = send_k[pl.ds(me * req_local, req_local)]

    def step(o, carry):
        slot = lax.rem(o, 2)
        load(o, slot).wait()
        norm_chip(o, slot)

        @pl.when(o + 2 < n_off)
        def _():
            load(o + 2, slot).start()

        c_copy(o, 0).start()
        c_copy(o, 1).start()
        return carry

    lax.fori_loop(1, n_off - 1, step, 0)

    last = n_off - 1
    slot = last % 2
    load(last, slot).wait()
    norm_chip(last, slot)
    c_copy(last, 1).start()
    c_out[:, pl.ds(pl.multiple_of(first_pos, 32), seq_local), :] = send_c[last, pl.ds(core * req_local, req_local)]

    def finish(o, carry):
        for copy in (c_copy, k_copy):
            for dc in range(CORES):
                copy(o, dc).wait_send()
                copy(o, dc).wait_recv()
        return carry

    lax.fori_loop(0, n_off - 1, finish, 0)
    for copy in (c_copy, k_copy):
        copy(last, 1).wait_send()
        copy(last, 1).wait_recv()


def attend_kernel(lens_s, c_in, k_in, q_lat, q_rope, c_out, k_out, o_out, k_turned, c_sem, k_sem):
    me = lax.axis_index("x")
    n_req, seq, width = c_in.shape
    rope = q_rope.shape[-1]
    heads = q_lat.shape[1]
    scale = (width + rope) ** -0.5
    pairs = 16

    def c_copy(r):
        return pltpu.make_async_copy(c_in.at[r], c_out.at[r], c_sem.at[r])

    def k_copy(r):
        return pltpu.make_async_copy(k_turned.at[r], k_out.at[r], k_sem.at[r])

    def start(r, carry):
        c_copy(r).start()
        return carry

    lax.fori_loop(0, n_req, start, 0)
    eye = (lax.broadcasted_iota(jnp.int32, (rope, 2 * rope), 0) == lax.rem(lax.broadcasted_iota(jnp.int32, (rope, 2 * rope), 1), rope)).astype(jnp.bfloat16)
    low_lane = lax.broadcasted_iota(jnp.int32, (1, 1, 2 * rope), 2) < rope

    def attend(r, carry):
        length = lens_s[me * n_req + r]
        both = k_in[r].reshape(seq // (2 * pairs), pairs, 2 * rope)
        zero = jnp.zeros_like(both)
        rows = jnp.concatenate([jnp.where(low_lane, both, zero)[:, None], jnp.where(low_lane, zero, both)[:, None]], axis=1).reshape(seq, 2 * rope)
        qr = q_rope[r]
        left = jnp.concatenate([jnp.concatenate([qr, qr], axis=1), eye], axis=0)
        turned = lax.dot_general(left, rows, (((1,), (1,)), ((), ())), preferred_element_type=jnp.float32)
        k_turned[r] = turned[heads:].astype(jnp.bfloat16)
        k_copy(r).start()
        c_req = c_in[r]
        scores = lax.dot_general(q_lat[r], c_req, (((1,), (1,)), ((), ())), preferred_element_type=jnp.float32)
        scores = (scores + turned[:heads]) * scale
        valid = lax.broadcasted_iota(jnp.int32, scores.shape, 1) < length
        scores = jnp.where(valid, scores, -1e30)
        weights = jnp.exp(scores - jnp.max(scores, axis=-1, keepdims=True))
        total = jnp.sum(weights, axis=-1, keepdims=True)
        mixed = jnp.dot(weights.astype(jnp.bfloat16), c_req, preferred_element_type=jnp.float32)
        o_out[r] = (mixed / total).astype(jnp.bfloat16)
        return carry

    lax.fori_loop(0, n_req, attend, 0)

    def finish(r, carry):
        c_copy(r).wait()
        k_copy(r).wait()
        return carry

    lax.fori_loop(0, n_req, finish, 0)


def solution(mesh):
    seq_spec = P("dp", "x", None)
    req_spec = P(("dp", "x"), None, None)
    vmem = pl.BlockSpec(memory_space=pltpu.VMEM)
    smem = pl.BlockSpec(memory_space=pltpu.SMEM)
    anywhere = pl.BlockSpec(memory_space=pl.ANY)

    def local_step(c_raw, k_raw, norm_gain, rope_cos, rope_sin, seq_lens, q_lat, q_rope):
        n_all, seq_local, width = c_raw.shape
        rope = k_raw.shape[-1]
        req_local, heads, _ = q_lat.shape
        n_dev = n_all // req_local
        seq = n_dev * seq_local
        pairs = seq_local // 2
        n_off = len(OFFSETS)
        lens_row = seq_lens.reshape(1, n_all)
        c_here, k_here = pl.pallas_call(
            exchange_kernel,
            out_shape=(pltpu.VMEM((req_local, seq, width), jnp.bfloat16), pltpu.VMEM((req_local, seq // 2, 2 * rope), jnp.bfloat16)),
            in_specs=[smem, anywhere, anywhere, vmem, vmem, vmem, vmem],
            out_specs=(vmem, vmem),
            scratch_shapes=[
                pltpu.VMEM((2, CORES * req_local, seq_local, width), jnp.bfloat16),
                pltpu.VMEM((n_off, CORES * req_local, seq_local, width), jnp.bfloat16),
                pltpu.VMEM((seq_local, rope, n_all), jnp.bfloat16),
                pltpu.VMEM((n_all * pairs, 2 * rope), jnp.float32),
                pltpu.VMEM((n_all, pairs, 2 * rope), jnp.bfloat16),
                pltpu.SemaphoreType.DMA((2,)),
                pltpu.SemaphoreType.DMA,
                pltpu.SemaphoreType.DMA((n_off, CORES)),
                pltpu.SemaphoreType.DMA((n_off, CORES)),
                pltpu.SemaphoreType.DMA((n_off, CORES)),
                pltpu.SemaphoreType.DMA((n_off, CORES)),
            ],
            compiler_params=pltpu.CompilerParams(collective_id=0, has_side_effects=True, vmem_limit_bytes=34 * MIB),
            name="exchange",
        )(seq_lens, c_raw, jnp.transpose(k_raw, (1, 2, 0)), norm_gain.reshape(1, width), rope_cos, rope_sin, lens_row)
        c_cache, k_turned, o_lat = pl.pallas_call(
            attend_kernel,
            out_shape=(
                jax.ShapeDtypeStruct((req_local, seq, width), jnp.bfloat16),
                jax.ShapeDtypeStruct((req_local, rope, seq), jnp.bfloat16),
                jax.ShapeDtypeStruct((req_local, heads, width), jnp.bfloat16),
            ),
            in_specs=[smem, vmem, vmem, vmem, vmem],
            out_specs=(anywhere, anywhere, vmem),
            scratch_shapes=[
                pltpu.VMEM((req_local, rope, seq), jnp.bfloat16),
                pltpu.SemaphoreType.DMA((req_local,)),
                pltpu.SemaphoreType.DMA((req_local,)),
            ],
            compiler_params=pltpu.CompilerParams(vmem_limit_bytes=16 * MIB),
            name="attend",
        )(seq_lens, c_here, k_here, q_lat, q_rope)
        return c_cache, jnp.transpose(k_turned, (0, 2, 1)), o_lat

    return jax.shard_map(local_step, mesh=mesh, in_specs=(seq_spec, seq_spec, P(None), P("x", None), P("x", None), P("dp"), req_spec, req_spec), out_specs=(req_spec, req_spec, req_spec), check_vma=False)
```

time: 318 us -> 260 us (0.82)
  the two profiles are of different devices: /device:TPU:107 before, /device:TPU:97 now
where the time goes in v1:
time: 260 us; the launch traced here: 255 us
  Pallas kernels  240 us (92%)
  local copies, waits for them, and re-layouts  14.8 us (6%)
    pallas_call x1, Pallas kernels, local_step(): pl.pallas_call(exchange_kernel, out_shape=(pltpu.VMEM((req_local, seq, wi...  225 us
    pallas_call x1, Pallas kernels, local_step(): pl.pallas_call(attend_kernel, out_shape=(jax.ShapeDtypeStruct((req_local,...  14.9 us
    unnamed x14, local copies, waits for them, and re-layouts  14 us

profile of v1, /device:TPU:97, one launch (start us, length us, event | category | flops | bytes accessed | tf_op | source)
XLA Modules:
  0.0 255.4 jit_solution(16965803636021901574)
XLA Ops:
  0.6 0.0 copy-start.3
  0.6 0.0 copy-start.2
  0.7 0.7 reshape.12.gain
  1.4 0.0 copy-start.4
  1.4 0.7 copy-done.4
  2.1 0.0 copy-start.5
  2.1 0.7 copy-done.5
  2.8 0.0 copy-start.6
  2.8 0.7 copy-done.6
  3.5 225.1 %exchange.1 = (bf16[16,1024,512]{2,1,0:T(8,128)(2,1)S(1)}, bf16[16,512,128]{2,1,0:T(8,128)(2,1)S(1)}) custom-call(s32[512]{0:T(512)S(1)} %copy-done.4, bf16[512,32,512]{2,1,0:T(8,128)(2,1)} %c_raw.1, bf16[32,64,512]{2,1,0:T(8,128)(2,1)} %bitcast.4, bf16[1,512]{1,0:T(2,128)(2,1)S(1)} %reshape.12.gain, f32[32,32]{1,0:T(8,128)S(1)} %copy-done.5, ...), custom_call_target="tpu_custom_call" | custom-call | tf_op jit(solution)/shard_map/exchange/pallas_call | solution.py:253
  228.6 0.0 copy-start
  228.6 6.2 %copy-done = bf16[16,1024,512]{2,1,0:T(8,128)(2,1)} copy-done((bf16[16,1024,512]{2,1,0:T(8,128)(2,1)}, bf16[16,1024,512]{2,1,0:T(8,128)(2,1)S(1)}, u32[]{:S(2)}) %copy-start) | copy-done | bytes 16777240
  234.7 0.0 copy-done.3
  234.7 0.0 copy-done.2
  234.7 0.0 copy-start.1
  234.8 5.8 %copy-done.1 = bf16[16,1024,512]{2,1,0:T(8,128)(2,1)S(1)} copy-done((bf16[16,1024,512]{2,1,0:T(8,128)(2,1)S(1)}, bf16[16,1024,512]{2,1,0:T(8,128)(2,1)}, u32[]{:S(2)}) %copy-start.1) | copy-done | bytes 16777240
  240.5 14.9 %attend.1 = (bf16[16,1024,512]{2,1,0:T(8,128)(2,1)}, bf16[16,64,1024]{2,1,0:T(8,128)(2,1)}, bf16[16,16,512]{2,1,0:T(8,128)(2,1)}) custom-call(s32[512]{0:T(512)S(1)} %copy-done.4, bf16[16,1024,512]{2,1,0:T(8,128)(2,1)S(1)} %copy-done.1, bf16[16,512,128]{2,1,0:T(8,128)(2,1)S(1)} %get-tuple-element.9.k_in, bf16[16,16,512]{2,1,0:T(8,128)(2,1)S(1)} %copy-done.2, ...), custom_call_target="tpu_custom_call" | custom-call | tf_op jit(solution)/shard_map/attend/pallas_call | solution.py:274
Async XLA Ops:
  0.6 234.1 %copy-start.3 = (bf16[16,16,64]{2,1,0:T(8,128)(2,1)S(1)}, bf16[16,16,64]{2,1,0:T(8,128)(2,1)}, u32[]{:S(2)}) copy-start(bf16[16,16,64]{2,1,0:T(8,128)(2,1)} %q_rope.1) | copy-start | bytes 98308
  0.6 234.1 %copy-start.2 = (bf16[16,16,512]{2,1,0:T(8,128)(2,1)S(1)}, bf16[16,16,512]{2,1,0:T(8,128)(2,1)}, u32[]{:S(2)}) copy-start(bf16[16,16,512]{2,1,0:T(8,128)(2,1)} %q_lat.1) | copy-start | bytes 786436
  1.4 0.7 copy-start.4
  2.1 0.7 copy-start.5
  2.8 0.7 copy-start.6
  228.6 6.2 %copy-start = (bf16[16,1024,512]{2,1,0:T(8,128)(2,1)}, bf16[16,1024,512]{2,1,0:T(8,128)(2,1)S(1)}, u32[]{:S(2)}) copy-start(bf16[16,1024,512]{2,1,0:T(8,128)(2,1)S(1)} %get-tuple-element.8.c_in) | copy-start | bytes 50331652
  234.7 5.8 %copy-start.1 = (bf16[16,1024,512]{2,1,0:T(8,128)(2,1)S(1)}, bf16[16,1024,512]{2,1,0:T(8,128)(2,1)}, u32[]{:S(2)}) copy-start(bf16[16,1024,512]{2,1,0:T(8,128)(2,1)} %copy-done) | copy-start | bytes 50331652

commit v2 on v1

v2 whole, which is shorter than its diff:
```python
import functools
import math

import jax
import jax.numpy as jnp
from jax import lax
from jax.experimental import pallas as pl
from jax.experimental.pallas import tpu as pltpu
from jax.sharding import PartitionSpec as P

NORM_EPS = 1e-6
MASKED = -1e30
MESH = pl.DeviceIdType.MESH
MIB = 2**20
CORES = 2
TOGETHER = 8

STAGES = (
    ((2, 2), (0, 0)),
    ((1, 1), (-1, -1)),
    ((1, -1), (-1, 1)),
    ((1, 2), (-1, 0)),
    ((-1, 2), (1, 0)),
    ((2, 1), (0, -1)),
    ((2, -1), (0, 1)),
    ((2, 0), (0, 2)),
)
OFFSETS = tuple(offset for stage in STAGES for offset in stage)
OWN = OFFSETS.index((0, 0))
NT = (((1,), (1,)), ((), ()))


def table(values, index):
    if isinstance(index, int):
        return values[index]
    out = jnp.int32(values[0])
    for place, value in enumerate(values[1:], 1):
        out = jnp.where(index == place, jnp.int32(value), out)
    return out


def chip_at(me, side, place, sign=1):
    chip = me // CORES
    dx = table([(sign * dx) % side for dx, _ in OFFSETS], place)
    dy = table([(sign * dy) % side for _, dy in OFFSETS], place)
    return lax.rem(chip // side + dy, side) * side + lax.rem(lax.rem(chip, side) + dx, side)


def stack_keys(pairs_rows):
    lanes = pairs_rows.shape[-1]
    low = lax.broadcasted_iota(jnp.int32, (1, 1, lanes), 2) < lanes // 2
    zero = jnp.zeros_like(pairs_rows)
    split = [jnp.where(low, pairs_rows, zero)[:, None], jnp.where(low, zero, pairs_rows)[:, None]]
    return jnp.concatenate(split, axis=1).reshape(-1, lanes)


def attend_stage(chips, lengths, queries, c_ref, k_ref, requests, seq_local, states):
    span = CORES * seq_local
    starts = [pl.multiple_of(chip * span, span) for chip in chips]
    rows = [jnp.concatenate([c_ref[r, pl.ds(start, span), :] for start in starts], axis=0) for r in requests]
    keys = [jnp.concatenate([stack_keys(k_ref[pl.ds(chip * CORES, CORES), r]) for chip in chips], axis=0) for r in requests]
    scale = (rows[0].shape[-1] + keys[0].shape[-1] // 2) ** -0.5
    scores = [lax.dot_general(q, jnp.concatenate([row, key], axis=1), NT, preferred_element_type=jnp.float32) for q, row, key in zip(queries, rows, keys)]
    lane = lax.broadcasted_iota(jnp.int32, scores[0].shape, 1)
    position = jnp.where(lane < span, starts[0] + lane, starts[1] - span + lane)
    scores = [jnp.where(position < length, score * scale, MASKED) for score, length in zip(scores, lengths)]
    tops = [jnp.maximum(state[0], jnp.max(score, axis=-1, keepdims=True)) for state, score in zip(states, scores)]
    keeps = [jnp.exp(state[0] - top) for state, top in zip(states, tops)]
    weights = [jnp.exp(score - top) for score, top in zip(scores, tops)]
    added = [jnp.dot(weight.astype(jnp.bfloat16), row, preferred_element_type=jnp.float32) for weight, row in zip(weights, rows)]
    out = []
    for (_, total, mixed), top, keep, weight, add in zip(states, tops, keeps, weights, added):
        wide_keep = jnp.concatenate([keep] * (mixed.shape[-1] // keep.shape[-1]), axis=1)
        out.append((top, total * keep + weight, mixed * wide_keep + add))
    return out


def exchange_kernel(
    side, lens_h, c_raw, k_raw, gain_h, cos_h, sin_h, q_lat_h, q_rope_h,
    c_out, k_out, top_out, total_out, mixed_out,
    lens_s, lens_v, gain, cos, sin, q_lat, q_rope, raw, send_c, k_in, k_rows, send_k,
    small_sem, raw_sem, k_sem, c_send, c_recv, k_send, k_recv,
):
    me = lax.axis_index("x")
    group = lax.axis_index("dp")
    core = lax.rem(me, CORES)
    n_dev = side * side * CORES
    n_off = len(OFFSETS)
    seq_local = c_raw.shape[1]
    req_local, heads, _ = q_lat.shape
    pair_req = CORES * req_local
    half = cos.shape[1]
    pairs = seq_local // 2
    first_pos = me * seq_local

    barrier = pltpu.get_barrier_semaphore()

    def greet(step, carry):
        pl.semaphore_signal(barrier, inc=1, device_id=(group, lax.rem(me + step, n_dev)), device_id_type=MESH)
        return carry

    lax.fori_loop(1, n_dev, greet, 0)

    def load(o, slot):
        return pltpu.make_async_copy(c_raw.at[pl.ds(chip_at(me, side, o) * pair_req, pair_req)], raw.at[slot], raw_sem.at[slot])

    def c_copy(o, dc):
        chip = chip_at(me, side, o)
        there = lax.rem(core + dc, CORES)
        return pltpu.make_async_remote_copy(
            send_c.at[o, pl.ds(there * req_local, req_local)],
            c_out.at[:, pl.ds(pl.multiple_of(first_pos, 32), seq_local), :],
            c_send.at[o, dc],
            c_recv.at[o, dc],
            device_id=(group, chip * CORES + there),
            device_id_type=MESH,
        )

    def k_copy(o, dc):
        chip = chip_at(me, side, o)
        there = lax.rem(core + dc, CORES)
        dest = chip * CORES + there
        return pltpu.make_async_remote_copy(
            send_k.at[pl.ds(dest * req_local, req_local)],
            k_out.at[me],
            k_send.at[o, dc],
            k_recv.at[o, dc],
            device_id=(group, dest),
            device_id_type=MESH,
        )

    def norm_chip(o, slot):
        first = chip_at(me, side, o) * pair_req
        scale = gain[...].astype(jnp.float32).reshape(1, gain.shape[0])

        def body(row, carry):
            length = lens_s[0, first + row]
            x = raw[slot, row].astype(jnp.float32)
            inv = lax.rsqrt(jnp.mean(x * x, axis=-1, keepdims=True) + NORM_EPS)
            valid = first_pos + lax.broadcasted_iota(jnp.int32, inv.shape, 0) < length
            send_c[o, row] = jnp.where(valid, x * inv * scale, 0.0).astype(jnp.bfloat16)
            return carry

        lax.fori_loop(0, pair_req, body, 0, unroll=4)

    small = [
        pltpu.make_async_copy(src, dst, small_sem.at[i])
        for i, (src, dst) in enumerate(((lens_h, lens_s), (gain_h, gain), (lens_h, lens_v), (cos_h, cos), (sin_h, sin), (q_lat_h, q_lat), (q_rope_h, q_rope)))
    ]
    k_load = pltpu.make_async_copy(k_raw, k_in, k_sem)
    load(0, 0).start()
    small[0].start()
    small[1].start()
    load(1, 1).start()
    k_load.start()
    for copy in small[2:]:
        copy.start()
    small[0].wait()
    small[1].wait()
    load(0, 0).wait()
    norm_chip(0, 0)
    load(2, 0).start()
    pl.semaphore_wait(barrier, n_dev - 1)
    c_copy(0, 0).start()
    c_copy(0, 1).start()

    for copy in small[2:]:
        copy.wait()
    k_load.wait()
    cos_t = cos[...].T
    sin_t = sin[...].T
    for pair in range(pairs):
        pieces = []
        for pos in (pair, pair + pairs):
            lo = k_in[pos, :half, :].astype(jnp.float32)
            hi = k_in[pos, half:, :].astype(jnp.float32)
            c = cos_t[:, pos : pos + 1]
            s = sin_t[:, pos : pos + 1]
            keep = first_pos + pos < lens_v[...]
            pieces.append(jnp.where(keep, lo * c - hi * s, 0.0))
            pieces.append(jnp.where(keep, hi * c + lo * s, 0.0))
        k_rows[pl.ds(pair, k_rows.shape[0] // pairs, stride=pairs), :] = jnp.concatenate(pieces, axis=0).T

    def pack(step, carry):
        rows = k_rows[pl.ds(pl.multiple_of(step * req_local * pairs, 256), req_local * pairs), :].astype(jnp.bfloat16)
        send_k[pl.ds(step * req_local, req_local)] = rows.reshape(req_local, pairs, k_rows.shape[1])
        return carry

    lax.fori_loop(0, n_dev, pack, 0)

    def start_k(o):
        @pl.when(o != OWN)
        def _():
            k_copy(o, 0).start()

        k_copy(o, 1).start()

    start_k(jnp.int32(0))
    k_out[me] = send_k[pl.ds(me * req_local, req_local)]

    def produce(o, carry):
        slot = lax.rem(o, 2)
        load(o, slot).wait()
        norm_chip(o, slot)

        @pl.when(o + 2 < n_off)
        def _():
            load(o + 2, slot).start()

        @pl.when(o != OWN)
        def _():
            c_copy(o, 0).start()

        c_copy(o, 1).start()

        start_k(o)
        return carry

    lax.fori_loop(1, n_off, produce, 0)
    c_out[:, pl.ds(pl.multiple_of(first_pos, 32), seq_local), :] = send_c[OWN, pl.ds(core * req_local, req_local)]

    def clear(r, carry):
        top_out[r] = jnp.full(top_out.shape[1:], MASKED, jnp.float32)
        total_out[r] = jnp.zeros(total_out.shape[1:], jnp.float32)
        mixed_out[r] = jnp.zeros(mixed_out.shape[1:], jnp.float32)
        return carry

    lax.fori_loop(0, req_local, clear, 0)

    def arrived(o):
        @pl.when(o != OWN)
        def _():
            c_copy(o, 0).wait_recv()
            k_copy(o, 0).wait_recv()

        c_copy(o, 1).wait_recv()
        k_copy(o, 1).wait_recv()

    def attend(stage, carry):
        chips = [chip_at(me, side, 2 * stage + i, -1) for i in range(2)]
        arrived(2 * stage)
        arrived(2 * stage + 1)

        def some(step, carry):
            requests = [step * TOGETHER + i for i in range(TOGETHER)]
            queries = [jnp.concatenate([q_lat[r], q_rope[r], q_rope[r]], axis=1) for r in requests]
            lengths = [lens_s[0, me * req_local + r] for r in requests]
            states = [(top_out[r], total_out[r], mixed_out[r]) for r in requests]
            states = attend_stage(chips, lengths, queries, c_out, k_out, requests, seq_local, states)
            for r, state in zip(requests, states):
                top_out[r], total_out[r], mixed_out[r] = state
            return carry

        lax.fori_loop(0, req_local // TOGETHER, some, 0)
        return carry

    lax.fori_loop(0, len(STAGES) - 1, attend, 0)
    arrived(jnp.int32(n_off - 2))
    arrived(jnp.int32(n_off - 1))

    def sent(o, carry):
        for copy in (c_copy, k_copy):

            @pl.when(o != OWN)
            def _():
                copy(o, 0).wait_send()

            copy(o, 1).wait_send()
        return carry

    lax.fori_loop(0, n_off, sent, 0)


def finish_kernel(side, lens_s, c_in, k_in, top, total, mixed, q_lat_h, q_rope_h, c_cache, k_cache, o_out, turned, q_lat, q_rope, c_sem, k_sem, q_sem):
    me = lax.axis_index("x")
    n_req, seq, _ = c_in.shape
    seq_local = seq // (side * side * CORES)
    n_off = len(OFFSETS)

    def c_copy(r):
        return pltpu.make_async_copy(c_in.at[r], c_cache.at[r], c_sem.at[r])

    q_copies = [pltpu.make_async_copy(src, dst, q_sem.at[i]) for i, (src, dst) in enumerate(((q_lat_h, q_lat), (q_rope_h, q_rope)))]
    for copy in q_copies:
        copy.start()

    def start(r, carry):
        c_copy(r).start()
        return carry

    lax.fori_loop(0, n_req, start, 0)
    k_copy = pltpu.make_async_copy(turned, k_cache, k_sem)
    rope = turned.shape[1]
    shape = (rope, 2 * rope)
    eye = (lax.broadcasted_iota(jnp.int32, shape, 0) == lax.rem(lax.broadcasted_iota(jnp.int32, shape, 1), rope)).astype(jnp.bfloat16)

    def turn(step, carry):
        requests = [step * 4 + i for i in range(4)]
        results = [lax.dot_general(eye, stack_keys(k_in[:, r]), NT, preferred_element_type=jnp.float32) for r in requests]
        for r, result in zip(requests, results):
            turned[r] = result.astype(jnp.bfloat16)
        return carry

    lax.fori_loop(0, n_req // 4, turn, 0)
    k_copy.start()
    for copy in q_copies:
        copy.wait()
    chips = [chip_at(me, side, n_off - 2 + i, -1) for i in range(2)]

    def some(step, carry):
        requests = [step * TOGETHER + i for i in range(TOGETHER)]
        queries = [jnp.concatenate([q_lat[r], q_rope[r], q_rope[r]], axis=1) for r in requests]
        lengths = [lens_s[me * n_req + r] for r in requests]
        states = [(top[r], total[r], mixed[r]) for r in requests]
        states = attend_stage(chips, lengths, queries, c_in, k_in, requests, seq_local, states)
        for r, (_, weights, values) in zip(requests, states):
            o_out[r] = (values / jnp.sum(weights, axis=-1, keepdims=True)).astype(jnp.bfloat16)
        return carry

    lax.fori_loop(0, n_req // TOGETHER, some, 0)

    def finish(r, carry):
        c_copy(r).wait()
        return carry

    lax.fori_loop(0, n_req, finish, 0)
    k_copy.wait()


def solution(mesh):
    seq_spec = P("dp", "x", None)
    req_spec = P(("dp", "x"), None, None)
    vmem = pl.BlockSpec(memory_space=pltpu.VMEM)
    smem = pl.BlockSpec(memory_space=pltpu.SMEM)
    anywhere = pl.BlockSpec(memory_space=pl.ANY)
    n_dev = mesh.shape["x"]
    side = math.isqrt(n_dev // CORES)

    def local_step(c_raw, k_raw, norm_gain, rope_cos, rope_sin, seq_lens, q_lat, q_rope):
        n_all, seq_local, width = c_raw.shape
        rope = k_raw.shape[-1]
        req_local, heads, _ = q_lat.shape
        seq = n_dev * seq_local
        pairs = seq_local // 2
        n_off = len(OFFSETS)
        lanes = 2 * CORES * seq_local
        state = pltpu.VMEM((req_local, heads, lanes), jnp.float32)
        received = pl.pallas_call(
            functools.partial(exchange_kernel, side),
            out_shape=(
                pltpu.VMEM((req_local, seq, width), jnp.bfloat16),
                pltpu.VMEM((n_dev, req_local, pairs, 2 * rope), jnp.bfloat16),
                state,
                state,
                pltpu.VMEM((req_local, heads, width), jnp.float32),
            ),
            in_specs=[anywhere] * 8,
            out_specs=(vmem,) * 5,
            scratch_shapes=[
                pltpu.SMEM((1, n_all), jnp.int32),
                pltpu.VMEM((1, n_all), jnp.int32),
                pltpu.VMEM((width,), jnp.bfloat16),
                pltpu.VMEM(rope_cos.shape, jnp.float32),
                pltpu.VMEM(rope_sin.shape, jnp.float32),
                pltpu.VMEM(q_lat.shape, jnp.bfloat16),
                pltpu.VMEM(q_rope.shape, jnp.bfloat16),
                pltpu.VMEM((2, CORES * req_local, seq_local, width), jnp.bfloat16),
                pltpu.VMEM((n_off, CORES * req_local, seq_local, width), jnp.bfloat16),
                pltpu.VMEM((seq_local, rope, n_all), jnp.bfloat16),
                pltpu.VMEM((n_all * pairs, 2 * rope), jnp.float32),
                pltpu.VMEM((n_all, pairs, 2 * rope), jnp.bfloat16),
                pltpu.SemaphoreType.DMA((7,)),
                pltpu.SemaphoreType.DMA((2,)),
                pltpu.SemaphoreType.DMA,
                pltpu.SemaphoreType.DMA((n_off, CORES)),
                pltpu.SemaphoreType.DMA((n_off, CORES)),
                pltpu.SemaphoreType.DMA((n_off, CORES)),
                pltpu.SemaphoreType.DMA((n_off, CORES)),
            ],
            compiler_params=pltpu.CompilerParams(collective_id=0, has_side_effects=True, vmem_limit_bytes=42 * MIB),
            name="exchange",
        )(seq_lens.reshape(1, n_all), c_raw, jnp.transpose(k_raw, (1, 2, 0)), norm_gain, rope_cos, rope_sin, q_lat, q_rope)
        c_cache, k_turned, o_lat = pl.pallas_call(
            functools.partial(finish_kernel, side),
            out_shape=(
                jax.ShapeDtypeStruct((req_local, seq, width), jnp.bfloat16),
                jax.ShapeDtypeStruct((req_local, rope, seq), jnp.bfloat16),
                jax.ShapeDtypeStruct((req_local, heads, width), jnp.bfloat16),
            ),
            in_specs=[smem] + [vmem] * 5 + [anywhere] * 2,
            out_specs=(anywhere, anywhere, vmem),
            scratch_shapes=[
                pltpu.VMEM((req_local, rope, seq), jnp.bfloat16),
                pltpu.VMEM(q_lat.shape, jnp.bfloat16),
                pltpu.VMEM(q_rope.shape, jnp.bfloat16),
                pltpu.SemaphoreType.DMA((req_local,)),
                pltpu.SemaphoreType.DMA,
                pltpu.SemaphoreType.DMA((2,)),
            ],
            compiler_params=pltpu.CompilerParams(vmem_limit_bytes=6 * MIB),
            name="finish",
        )(seq_lens, *received, q_lat, q_rope)
        return c_cache, jnp.transpose(k_turned, (0, 2, 1)), o_lat

    return jax.shard_map(local_step, mesh=mesh, in_specs=(seq_spec, seq_spec, P(None), P("x", None), P("x", None), P("dp"), req_spec, req_spec), out_specs=(req_spec, req_spec, req_spec), check_vma=False)
```

time: 260 us -> 231 us (0.89)
  the two profiles are of different devices: /device:TPU:97 before, /device:TPU:99 now
where the time goes in v2:
time: 231 us
  Pallas kernels  230 us (100%)
    pallas_call x1, Pallas kernels, local_step(): pl.pallas_call(functools.partial(exchange_kernel, side), out_shape=(pltpu...  222 us
    pallas_call x1, Pallas kernels, local_step(): pl.pallas_call(functools.partial(finish_kernel, side), out_shape=(jax.Sha...  8.03 us

profile of v2, /device:TPU:99, one launch (start us, length us, event | category | flops | bytes accessed | tf_op | source)
XLA Modules:
  0.0 231.0 jit_solution(18050142536421095471)
XLA Ops:
  0.6 0.0 copy-start.1
  0.6 0.0 copy-start
  0.7 0.0 copy-start.2
  0.7 222.3 %exchange.1 = (bf16[16,1024,512]{2,1,0:T(8,128)(2,1)S(1)}, bf16[32,16,16,128]{3,2,1,0:T(8,128)(2,1)S(1)}, f32[16,16,128]{2,1,0:T(8,128)S(1)}, f32[16,16,128]{2,1,0:T(8,128)S(1)}, f32[16,16,512]{2,1,0:T(8,128)S(1)}) custom-call(s32[1,512]{1,0:T(1,128)} %bitcast.3, bf16[512,32,512]{2,1,0:T(8,128)(2,1)} %c_raw.1, bf16[32,64,512]{2,1,0:T(8,128)(2,1)} %bitcast.4, ...), custom_call_target="tpu_custom_call" | custom-call | tf_op jit(solution)/shard_map/exchange/pallas_call | solution.py:348
  222.9 0.0 copy-done.1
  223.0 0.0 copy-done
  223.0 0.0 copy-done.2
  223.0 8.0 %finish.1 = (bf16[16,1024,512]{2,1,0:T(8,128)(2,1)}, bf16[16,64,1024]{2,1,0:T(8,128)(2,1)}, bf16[16,16,512]{2,1,0:T(8,128)(2,1)}) custom-call(s32[512]{0:T(512)S(1)} %copy-done.2, bf16[16,1024,512]{2,1,0:T(8,128)(2,1)S(1)} %get-tuple-element.11.c_in, bf16[32,16,16,128]{3,2,1,0:T(8,128)(2,1)S(1)} %get-tuple-element.12.k_in, ...), custom_call_target="tpu_custom_call" | custom-call | tf_op jit(solution)/shard_map/finish/pallas_call | solution.py:383
Async XLA Ops:
  0.6 222.3 %copy-start.1 = (bf16[16,16,64]{2,1,0:T(8,128)(2,1)S(1)}, bf16[16,16,64]{2,1,0:T(8,128)(2,1)}, u32[]{:S(2)}) copy-start(bf16[16,16,64]{2,1,0:T(8,128)(2,1)} %q_rope_h.3) | copy-start | bytes 98308
  0.6 222.3 %copy-start = (bf16[16,16,512]{2,1,0:T(8,128)(2,1)S(1)}, bf16[16,16,512]{2,1,0:T(8,128)(2,1)}, u32[]{:S(2)}) copy-start(bf16[16,16,512]{2,1,0:T(8,128)(2,1)} %q_lat_h.3) | copy-start | bytes 786436
  0.7 222.3 %copy-start.2 = (s32[512]{0:T(512)S(1)}, s32[512]{0:T(512)}, u32[]{:S(2)}) copy-start(s32[512]{0:T(512)} %lens_s.1) | copy-start | bytes 6148

commit v3 on v2

--- a/solution.py
+++ b/solution.py
@@ -27,6 +27,8 @@
 )
 OFFSETS = tuple(offset for stage in STAGES for offset in stage)
 OWN = OFFSETS.index((0, 0))
+EARLY = ((0, 1), (2, 3), (4, 5), (6, 7), (9, 10), (11, 12))
+LATE = ((8, 13), (14, 15))
 NT = (((1,), (1,)), ((), ()))
 
 
@@ -237,9 +239,10 @@
         k_copy(o, 1).wait_recv()
 
     def attend(stage, carry):
-        chips = [chip_at(me, side, 2 * stage + i, -1) for i in range(2)]
-        arrived(2 * stage)
-        arrived(2 * stage + 1)
+        places = [table([pair[i] for pair in EARLY], stage) for i in range(2)]
+        chips = [chip_at(me, side, place, -1) for place in places]
+        for place in places:
+            arrived(place)
 
         def some(step, carry):
             requests = [step * TOGETHER + i for i in range(TOGETHER)]
@@ -254,9 +257,10 @@
         lax.fori_loop(0, req_local // TOGETHER, some, 0)
         return carry
 
-    lax.fori_loop(0, len(STAGES) - 1, attend, 0)
-    arrived(jnp.int32(n_off - 2))
-    arrived(jnp.int32(n_off - 1))
+    lax.fori_loop(0, len(EARLY), attend, 0)
+    for pair in LATE:
+        for place in pair:
+            arrived(jnp.int32(place))
 
     def sent(o, carry):
         for copy in (c_copy, k_copy):
@@ -271,24 +275,23 @@
     lax.fori_loop(0, n_off, sent, 0)
 
 
-def finish_kernel(side, lens_s, c_in, k_in, top, total, mixed, q_lat_h, q_rope_h, c_cache, k_cache, o_out, turned, q_lat, q_rope, c_sem, k_sem, q_sem):
+def finish_kernel(side, lens_h, c_in, k_in, top, total, mixed, q_lat_h, q_rope_h, c_cache, k_cache, o_lat, lens_s, turned, q_lat, q_rope, o_here, c_sem, k_sem, o_sem, small_sem):
     me = lax.axis_index("x")
     n_req, seq, _ = c_in.shape
     seq_local = seq // (side * side * CORES)
-    n_off = len(OFFSETS)
 
     def c_copy(r):
         return pltpu.make_async_copy(c_in.at[r], c_cache.at[r], c_sem.at[r])
 
-    q_copies = [pltpu.make_async_copy(src, dst, q_sem.at[i]) for i, (src, dst) in enumerate(((q_lat_h, q_lat), (q_rope_h, q_rope)))]
-    for copy in q_copies:
-        copy.start()
-
     def start(r, carry):
         c_copy(r).start()
         return carry
 
+    small = [pltpu.make_async_copy(src, dst, small_sem.at[i]) for i, (src, dst) in enumerate(((lens_h, lens_s), (q_lat_h, q_lat), (q_rope_h, q_rope)))]
+    for copy in small:
+        copy.start()
     lax.fori_loop(0, n_req, start, 0)
+
     k_copy = pltpu.make_async_copy(turned, k_cache, k_sem)
     rope = turned.shape[1]
     shape = (rope, 2 * rope)
@@ -303,21 +306,24 @@
 
     lax.fori_loop(0, n_req // 4, turn, 0)
     k_copy.start()
-    for copy in q_copies:
+    for copy in small:
         copy.wait()
-    chips = [chip_at(me, side, n_off - 2 + i, -1) for i in range(2)]
 
     def some(step, carry):
         requests = [step * TOGETHER + i for i in range(TOGETHER)]
         queries = [jnp.concatenate([q_lat[r], q_rope[r], q_rope[r]], axis=1) for r in requests]
-        lengths = [lens_s[me * n_req + r] for r in requests]
+        lengths = [lens_s[0, me * n_req + r] for r in requests]
         states = [(top[r], total[r], mixed[r]) for r in requests]
-        states = attend_stage(chips, lengths, queries, c_in, k_in, requests, seq_local, states)
+        for pair in LATE:
+            chips = [chip_at(me, side, place, -1) for place in pair]
+            states = attend_stage(chips, lengths, queries, c_in, k_in, requests, seq_local, states)
         for r, (_, weights, values) in zip(requests, states):
-            o_out[r] = (values / jnp.sum(weights, axis=-1, keepdims=True)).astype(jnp.bfloat16)
+            o_here[r] = (values / jnp.sum(weights, axis=-1, keepdims=True)).astype(jnp.bfloat16)
         return carry
 
     lax.fori_loop(0, n_req // TOGETHER, some, 0)
+    o_copy = pltpu.make_async_copy(o_here, o_lat, o_sem)
+    o_copy.start()
 
     def finish(r, carry):
         c_copy(r).wait()
@@ -325,13 +331,13 @@
 
     lax.fori_loop(0, n_req, finish, 0)
     k_copy.wait()
+    o_copy.wait()
 
 
 def solution(mesh):
     seq_spec = P("dp", "x", None)
     req_spec = P(("dp", "x"), None, None)
     vmem = pl.BlockSpec(memory_space=pltpu.VMEM)
-    smem = pl.BlockSpec(memory_space=pltpu.SMEM)
     anywhere = pl.BlockSpec(memory_space=pl.ANY)
     n_dev = mesh.shape["x"]
     side = math.isqrt(n_dev // CORES)
@@ -344,6 +350,7 @@
         pairs = seq_local // 2
         n_off = len(OFFSETS)
         lanes = 2 * CORES * seq_local
+        lens_row = seq_lens.reshape(1, n_all)
         state = pltpu.VMEM((req_local, heads, lanes), jnp.float32)
         received = pl.pallas_call(
             functools.partial(exchange_kernel, side),
@@ -379,7 +386,7 @@
             ],
             compiler_params=pltpu.CompilerParams(collective_id=0, has_side_effects=True, vmem_limit_bytes=42 * MIB),
             name="exchange",
-        )(seq_lens.reshape(1, n_all), c_raw, jnp.transpose(k_raw, (1, 2, 0)), norm_gain, rope_cos, rope_sin, q_lat, q_rope)
+        )(lens_row, c_raw, jnp.transpose(k_raw, (1, 2, 0)), norm_gain, rope_cos, rope_sin, q_lat, q_rope)
         c_cache, k_turned, o_lat = pl.pallas_call(
             functools.partial(finish_kernel, side),
             out_shape=(
@@ -387,19 +394,22 @@
                 jax.ShapeDtypeStruct((req_local, rope, seq), jnp.bfloat16),
                 jax.ShapeDtypeStruct((req_local, heads, width), jnp.bfloat16),
             ),
-            in_specs=[smem] + [vmem] * 5 + [anywhere] * 2,
-            out_specs=(anywhere, anywhere, vmem),
+            in_specs=[anywhere] + [vmem] * 5 + [anywhere] * 2,
+            out_specs=(anywhere, anywhere, anywhere),
             scratch_shapes=[
+                pltpu.SMEM((1, n_all), jnp.int32),
                 pltpu.VMEM((req_local, rope, seq), jnp.bfloat16),
                 pltpu.VMEM(q_lat.shape, jnp.bfloat16),
                 pltpu.VMEM(q_rope.shape, jnp.bfloat16),
+                pltpu.VMEM(q_lat.shape, jnp.bfloat16),
                 pltpu.SemaphoreType.DMA((req_local,)),
                 pltpu.SemaphoreType.DMA,
-                pltpu.SemaphoreType.DMA((2,)),
+                pltpu.SemaphoreType.DMA,
+                pltpu.SemaphoreType.DMA((3,)),
             ],
             compiler_params=pltpu.CompilerParams(vmem_limit_bytes=6 * MIB),
             name="finish",
-        )(seq_lens, *received, q_lat, q_rope)
+        )(lens_row, *received, q_lat, q_rope)
         return c_cache, jnp.transpose(k_turned, (0, 2, 1)), o_lat
 
     return jax.shard_map(local_step, mesh=mesh, in_specs=(seq_spec, seq_spec, P(None), P("x", None), P("x", None), P("dp"), req_spec, req_spec), out_specs=(req_spec, req_spec, req_spec), check_vma=False)

time: 231 us -> 226 us (0.978)
  the two profiles are of different devices: /device:TPU:99 before, /device:TPU:97 now
where the time goes in v3:
time: 226 us; the launch traced here: 224 us
  Pallas kernels  224 us (99%)
    pallas_call x1, Pallas kernels, local_step(): pl.pallas_call(functools.partial(exchange_kernel, side), out_shape=(pltpu...  217 us
    pallas_call x1, Pallas kernels, local_step(): pl.pallas_call(functools.partial(finish_kernel, side), out_shape=(jax.Sha...  6.79 us

profile of v3, /device:TPU:97, one launch (start us, length us, event | category | flops | bytes accessed | tf_op | source)
XLA Modules:
  0.0 224.5 jit_solution(15992240142243661003)
XLA Ops:
  0.6 0.0 copy-start.1
  0.6 0.0 copy-start
  0.7 0.0 copy-start.2
  0.7 217.0 %exchange.1 = (bf16[16,1024,512]{2,1,0:T(8,128)(2,1)S(1)}, bf16[32,16,16,128]{3,2,1,0:T(8,128)(2,1)S(1)}, f32[16,16,128]{2,1,0:T(8,128)S(1)}, f32[16,16,128]{2,1,0:T(8,128)S(1)}, f32[16,16,512]{2,1,0:T(8,128)S(1)}) custom-call(s32[1,512]{1,0:T(1,128)} %bitcast.3, bf16[512,32,512]{2,1,0:T(8,128)(2,1)} %c_raw.1, bf16[32,64,512]{2,1,0:T(8,128)(2,1)} %bitcast.5, ...), custom_call_target="tpu_custom_call" | custom-call | tf_op jit(solution)/shard_map/exchange/pallas_call | solution.py:355
  217.6 0.0 copy-done.1
  217.6 0.0 copy-done
  217.7 0.0 copy-done.2
  217.7 6.8 %finish.1 = (bf16[16,1024,512]{2,1,0:T(8,128)(2,1)}, bf16[16,64,1024]{2,1,0:T(8,128)(2,1)}, bf16[16,16,512]{2,1,0:T(8,128)(2,1)}) custom-call(s32[1,512]{1,0:T(1,128)S(1)} %bitcast.4, bf16[16,1024,512]{2,1,0:T(8,128)(2,1)S(1)} %get-tuple-element.11.c_in, bf16[32,16,16,128]{3,2,1,0:T(8,128)(2,1)S(1)} %get-tuple-element.12.k_in, ...), custom_call_target="tpu_custom_call" | custom-call | tf_op jit(solution)/shard_map/finish/pallas_call | solution.py:390
Async XLA Ops:
  0.6 217.0 %copy-start.1 = (bf16[16,16,64]{2,1,0:T(8,128)(2,1)S(1)}, bf16[16,16,64]{2,1,0:T(8,128)(2,1)}, u32[]{:S(2)}) copy-start(bf16[16,16,64]{2,1,0:T(8,128)(2,1)} %q_rope_h.3) | copy-start | bytes 98308
  0.6 217.0 %copy-start = (bf16[16,16,512]{2,1,0:T(8,128)(2,1)S(1)}, bf16[16,16,512]{2,1,0:T(8,128)(2,1)}, u32[]{:S(2)}) copy-start(bf16[16,16,512]{2,1,0:T(8,128)(2,1)} %q_lat_h.3) | copy-start | bytes 786436
  0.7 217.0 %copy-start.2 = (s32[512]{0:T(512)S(1)}, s32[512]{0:T(512)}, u32[]{:S(2)}) copy-start(s32[512]{0:T(512)} %param.13) | copy-start | bytes 6148

commit v4 on v3

--- a/solution.py
+++ b/solution.py
@@ -17,18 +17,18 @@
 
 STAGES = (
     ((2, 2), (0, 0)),
+    ((2, -1), (0, 1)),
+    ((2, 1), (0, -1)),
+    ((2, 0), (0, 2)),
+    ((1, 2), (-1, 0)),
+    ((-1, 2), (1, 0)),
     ((1, 1), (-1, -1)),
     ((1, -1), (-1, 1)),
-    ((1, 2), (-1, 0)),
-    ((-1, 2), (1, 0)),
-    ((2, 1), (0, -1)),
-    ((2, -1), (0, 1)),
-    ((2, 0), (0, 2)),
 )
 OFFSETS = tuple(offset for stage in STAGES for offset in stage)
 OWN = OFFSETS.index((0, 0))
-EARLY = ((0, 1), (2, 3), (4, 5), (6, 7), (9, 10), (11, 12))
-LATE = ((8, 13), (14, 15))
+EARLY = ((0, 1), (2, 3), (4, 5), (6, 7), (8, 9), (10, 11))
+LATE = ((12, 13), (14, 15))
 NT = (((1,), (1,)), ((), ()))
 
 
@@ -79,9 +79,9 @@
 
 def exchange_kernel(
     side, lens_h, c_raw, k_raw, gain_h, cos_h, sin_h, q_lat_h, q_rope_h,
-    c_out, k_out, top_out, total_out, mixed_out,
-    lens_s, lens_v, gain, cos, sin, q_lat, q_rope, raw, send_c, k_in, k_rows, send_k,
-    small_sem, raw_sem, k_sem, c_send, c_recv, k_send, k_recv,
+    c_out, k_out, top_out, total_out, mixed_out, lens_v, q_lat, q_rope,
+    lens_s, gain, cos, sin, raw, send_c, k_in, k_rows, send_k,
+    small_sem, half_sem, raw_sem, k_sem, c_send, c_recv, k_send, k_recv,
 ):
     me = lax.axis_index("x")
     group = lax.axis_index("dp")
@@ -101,10 +101,12 @@
         pl.semaphore_signal(barrier, inc=1, device_id=(group, lax.rem(me + step, n_dev)), device_id_type=MESH)
         return carry
 
-    lax.fori_loop(1, n_dev, greet, 0)
-
     def load(o, slot):
         return pltpu.make_async_copy(c_raw.at[pl.ds(chip_at(me, side, o) * pair_req, pair_req)], raw.at[slot], raw_sem.at[slot])
+
+    def load_half(dc):
+        there = lax.rem(core + dc, CORES) * req_local
+        return pltpu.make_async_copy(c_raw.at[pl.ds(chip_at(me, side, 0) * pair_req + there, req_local)], raw.at[0, pl.ds(there, req_local)], half_sem.at[dc])
 
     def c_copy(o, dc):
         chip = chip_at(me, side, o)
@@ -131,11 +133,12 @@
             device_id_type=MESH,
         )
 
-    def norm_chip(o, slot):
+    def norm_rows(o, slot, start, count):
         first = chip_at(me, side, o) * pair_req
         scale = gain[...].astype(jnp.float32).reshape(1, gain.shape[0])
 
-        def body(row, carry):
+        def body(step, carry):
+            row = start + step
             length = lens_s[0, first + row]
             x = raw[slot, row].astype(jnp.float32)
             inv = lax.rsqrt(jnp.mean(x * x, axis=-1, keepdims=True) + NORM_EPS)
@@ -143,28 +146,32 @@
             send_c[o, row] = jnp.where(valid, x * inv * scale, 0.0).astype(jnp.bfloat16)
             return carry
 
-        lax.fori_loop(0, pair_req, body, 0, unroll=4)
+        lax.fori_loop(0, count, body, 0, unroll=4)
 
     small = [
         pltpu.make_async_copy(src, dst, small_sem.at[i])
         for i, (src, dst) in enumerate(((lens_h, lens_s), (gain_h, gain), (lens_h, lens_v), (cos_h, cos), (sin_h, sin), (q_lat_h, q_lat), (q_rope_h, q_rope)))
     ]
     k_load = pltpu.make_async_copy(k_raw, k_in, k_sem)
-    load(0, 0).start()
+    load_half(0).start()
     small[0].start()
     small[1].start()
+    lax.fori_loop(1, n_dev, greet, 0)
+    load_half(1).start()
     load(1, 1).start()
     k_load.start()
     for copy in small[2:]:
         copy.start()
     small[0].wait()
     small[1].wait()
-    load(0, 0).wait()
-    norm_chip(0, 0)
-    load(2, 0).start()
+    load_half(0).wait()
+    norm_rows(0, 0, core * req_local, req_local)
     pl.semaphore_wait(barrier, n_dev - 1)
     c_copy(0, 0).start()
+    load_half(1).wait()
+    norm_rows(0, 0, (CORES - 1 - core) * req_local, req_local)
     c_copy(0, 1).start()
+    load(2, 0).start()
 
     for copy in small[2:]:
         copy.wait()
@@ -203,7 +210,7 @@
     def produce(o, carry):
         slot = lax.rem(o, 2)
         load(o, slot).wait()
-        norm_chip(o, slot)
+        norm_rows(o, slot, 0, pair_req)
 
         @pl.when(o + 2 < n_off)
         def _():
@@ -275,7 +282,7 @@
     lax.fori_loop(0, n_off, sent, 0)
 
 
-def finish_kernel(side, lens_h, c_in, k_in, top, total, mixed, q_lat_h, q_rope_h, c_cache, k_cache, o_lat, lens_s, turned, q_lat, q_rope, o_here, c_sem, k_sem, o_sem, small_sem):
+def finish_kernel(side, c_in, k_in, top, total, mixed, lens_v, q_lat, q_rope, c_cache, k_cache, o_lat, lens_s, turned, o_here, c_sem, k_sem, o_sem, lens_sem):
     me = lax.axis_index("x")
     n_req, seq, _ = c_in.shape
     seq_local = seq // (side * side * CORES)
@@ -287,9 +294,8 @@
         c_copy(r).start()
         return carry
 
-    small = [pltpu.make_async_copy(src, dst, small_sem.at[i]) for i, (src, dst) in enumerate(((lens_h, lens_s), (q_lat_h, q_lat), (q_rope_h, q_rope)))]
-    for copy in small:
-        copy.start()
+    lens_copy = pltpu.make_async_copy(lens_v, lens_s, lens_sem)
+    lens_copy.start()
     lax.fori_loop(0, n_req, start, 0)
 
     k_copy = pltpu.make_async_copy(turned, k_cache, k_sem)
@@ -306,8 +312,7 @@
 
     lax.fori_loop(0, n_req // 4, turn, 0)
     k_copy.start()
-    for copy in small:
-        copy.wait()
+    lens_copy.wait()
 
     def some(step, carry):
         requests = [step * TOGETHER + i for i in range(TOGETHER)]
@@ -360,23 +365,24 @@
                 state,
                 state,
                 pltpu.VMEM((req_local, heads, width), jnp.float32),
+                pltpu.VMEM((1, n_all), jnp.int32),
+                pltpu.VMEM(q_lat.shape, jnp.bfloat16),
+                pltpu.VMEM(q_rope.shape, jnp.bfloat16),
             ),
             in_specs=[anywhere] * 8,
-            out_specs=(vmem,) * 5,
+            out_specs=(vmem,) * 8,
             scratch_shapes=[
                 pltpu.SMEM((1, n_all), jnp.int32),
-                pltpu.VMEM((1, n_all), jnp.int32),
                 pltpu.VMEM((width,), jnp.bfloat16),
                 pltpu.VMEM(rope_cos.shape, jnp.float32),
                 pltpu.VMEM(rope_sin.shape, jnp.float32),
-                pltpu.VMEM(q_lat.shape, jnp.bfloat16),
-                pltpu.VMEM(q_rope.shape, jnp.bfloat16),
                 pltpu.VMEM((2, CORES * req_local, seq_local, width), jnp.bfloat16),
                 pltpu.VMEM((n_off, CORES * req_local, seq_local, width), jnp.bfloat16),
                 pltpu.VMEM((seq_local, rope, n_all), jnp.bfloat16),
                 pltpu.VMEM((n_all * pairs, 2 * rope), jnp.float32),
                 pltpu.VMEM((n_all, pairs, 2 * rope), jnp.bfloat16),
                 pltpu.SemaphoreType.DMA((7,)),
+                pltpu.SemaphoreType.DMA((CORES,)),
                 pltpu.SemaphoreType.DMA((2,)),
                 pltpu.SemaphoreType.DMA,
                 pltpu.SemaphoreType.DMA((n_off, CORES)),
@@ -394,22 +400,20 @@
                 jax.ShapeDtypeStruct((req_local, rope, seq), jnp.bfloat16),
                 jax.ShapeDtypeStruct((req_local, heads, width), jnp.bfloat16),
             ),
-            in_specs=[anywhere] + [vmem] * 5 + [anywhere] * 2,
+            in_specs=[vmem] * 8,
             out_specs=(anywhere, anywhere, anywhere),
             scratch_shapes=[
                 pltpu.SMEM((1, n_all), jnp.int32),
                 pltpu.VMEM((req_local, rope, seq), jnp.bfloat16),
                 pltpu.VMEM(q_lat.shape, jnp.bfloat16),
-                pltpu.VMEM(q_rope.shape, jnp.bfloat16),
-                pltpu.VMEM(q_lat.shape, jnp.bfloat16),
                 pltpu.SemaphoreType.DMA((req_local,)),
                 pltpu.SemaphoreType.DMA,
                 pltpu.SemaphoreType.DMA,
-                pltpu.SemaphoreType.DMA((3,)),
+                pltpu.SemaphoreType.DMA,
             ],
             compiler_params=pltpu.CompilerParams(vmem_limit_bytes=6 * MIB),
             name="finish",
-        )(lens_row, *received, q_lat, q_rope)
+        )(*received)
         return c_cache, jnp.transpose(k_turned, (0, 2, 1)), o_lat
 
     return jax.shard_map(local_step, mesh=mesh, in_specs=(seq_spec, seq_spec, P(None), P("x", None), P("x", None), P("dp"), req_spec, req_spec), out_specs=(req_spec, req_spec, req_spec), check_vma=False)

time: 226 us -> 224 us (level)
  no operation moved by 1% of the time
where the time goes in v4:
time: 224 us
  Pallas kernels  223 us (100%)
    pallas_call x1, Pallas kernels, local_step(): pl.pallas_call(functools.partial(exchange_kernel, side), out_shape=(pltpu...  216 us
    pallas_call x1, Pallas kernels, local_step(): pl.pallas_call(functools.partial(finish_kernel, side), out_shape=(jax.Sha...  6.68 us

profile of v4, /device:TPU:97, one launch (start us, length us, event | category | flops | bytes accessed | tf_op | source)
XLA Modules:
  0.0 223.6 jit_solution(14690160788655526015)
XLA Ops:
  0.6 216.3 %exchange.1 = (bf16[16,1024,512]{2,1,0:T(8,128)(2,1)S(1)}, bf16[32,16,16,128]{3,2,1,0:T(8,128)(2,1)S(1)}, f32[16,16,128]{2,1,0:T(8,128)S(1)}, f32[16,16,128]{2,1...) custom-call(s32[1,512]{1,0:T(1,128)} %bitcast.4, ...), custom_call_target="tpu_custom_call" | custom-call | tf_op jit(solution)/shard_map/exchange/pallas_call | solution.py:360
  216.9 6.7 %finish.1 = (bf16[16,1024,512]{2,1,0:T(8,128)(2,1)}, bf16[16,64,1024]{2,1,0:T(8,128)(2,1)}, bf16[16,16,512]{2,1,0:T(8,128)(2,1)}) custom-call(bf16[16,1024,512]{2,1,0:T(8,128)(2,1)S(1)} %get-tuple-element.14.c_in, bf16[32,16,16,128]{3,2,1,0:T(8,128)(2,1)S(1)} %get-tuple-element.15.k_in, f32[16,16,128]{2,1,0:T(8,128)S(1)} %get-tuple-element.16.top, ...), custom_call_target="tpu_custom_call" | custom-call | tf_op jit(solution)/shard_map/finish/pallas_call | solution.py:396

commit v5 on v4

--- a/solution.py
+++ b/solution.py
@@ -265,9 +265,6 @@
         return carry
 
     lax.fori_loop(0, len(EARLY), attend, 0)
-    for pair in LATE:
-        for place in pair:
-            arrived(jnp.int32(place))
 
     def sent(o, carry):
         for copy in (c_copy, k_copy):
@@ -280,6 +277,11 @@
         return carry
 
     lax.fori_loop(0, n_off, sent, 0)
+    for pair in LATE:
+        for place in pair:
+            for dc in range(CORES):
+                k_copy(place, dc).wait_recv()
+                c_copy(place, dc).wait_recv()
 
 
 def finish_kernel(side, c_in, k_in, top, total, mixed, lens_v, q_lat, q_rope, c_cache, k_cache, o_lat, lens_s, turned, o_here, c_sem, k_sem, o_sem, lens_sem):

time: 224 us -> 224 us (level)
  no operation moved by 1% of the time
where the time goes in v5:
time: 224 us; the launch traced here: 223 us
  Pallas kernels  223 us (100%)
    pallas_call x1, Pallas kernels, local_step(): pl.pallas_call(functools.partial(exchange_kernel, side), out_shape=(pltpu...  216 us
    pallas_call x1, Pallas kernels, local_step(): pl.pallas_call(functools.partial(finish_kernel, side), out_shape=(jax.Sha...  6.68 us

profile of v5, /device:TPU:97, one launch (start us, length us, event | category | flops | bytes accessed | tf_op | source)
XLA Modules:
  0.0 223.4 jit_solution(18110756991440042209)
XLA Ops:
  0.6 216.1 %exchange.1 = (bf16[16,1024,512]{2,1,0:T(8,128)(2,1)S(1)}, bf16[32,16,16,128]{3,2,1,0:T(8,128)(2,1)S(1)}, f32[16,16,128]{2,1,0:T(8,128)S(1)}, f32[16,16,128]{2,1...) custom-call(s32[1,512]{1,0:T(1,128)} %bitcast.4, ...), custom_call_target="tpu_custom_call" | custom-call | tf_op jit(solution)/shard_map/exchange/pallas_call | solution.py:362
  216.8 6.7 %finish.1 = (bf16[16,1024,512]{2,1,0:T(8,128)(2,1)}, bf16[16,64,1024]{2,1,0:T(8,128)(2,1)}, bf16[16,16,512]{2,1,0:T(8,128)(2,1)}) custom-call(bf16[16,1024,512]{2,1,0:T(8,128)(2,1)S(1)} %get-tuple-element.14.c_in, bf16[32,16,16,128]{3,2,1,0:T(8,128)(2,1)S(1)} %get-tuple-element.15.k_in, f32[16,16,128]{2,1,0:T(8,128)S(1)} %get-tuple-element.16.top, ...), custom_call_target="tpu_custom_call" | custom-call | tf_op jit(solution)/shard_map/finish/pallas_call | solution.py:398

commit v6 on v5

--- a/solution.py
+++ b/solution.py
@@ -14,6 +14,7 @@
 MIB = 2**20
 CORES = 2
 TOGETHER = 8
+COPIED = 4
 
 STAGES = (
     ((2, 2), (0, 0)),
@@ -290,7 +291,8 @@
     seq_local = seq // (side * side * CORES)
 
     def c_copy(r):
-        return pltpu.make_async_copy(c_in.at[r], c_cache.at[r], c_sem.at[r])
+        some_requests = pl.ds(r * COPIED, COPIED)
+        return pltpu.make_async_copy(c_in.at[some_requests], c_cache.at[some_requests], c_sem.at[r])
 
     def start(r, carry):
         c_copy(r).start()
@@ -298,7 +300,7 @@
 
     lens_copy = pltpu.make_async_copy(lens_v, lens_s, lens_sem)
     lens_copy.start()
-    lax.fori_loop(0, n_req, start, 0)
+    lax.fori_loop(0, n_req // COPIED, start, 0)
 
     k_copy = pltpu.make_async_copy(turned, k_cache, k_sem)
     rope = turned.shape[1]
@@ -336,7 +338,7 @@
         c_copy(r).wait()
         return carry
 
-    lax.fori_loop(0, n_req, finish, 0)
+    lax.fori_loop(0, n_req // COPIED, finish, 0)
     k_copy.wait()
     o_copy.wait()
 
@@ -408,7 +410,7 @@
                 pltpu.SMEM((1, n_all), jnp.int32),
                 pltpu.VMEM((req_local, rope, seq), jnp.bfloat16),
                 pltpu.VMEM(q_lat.shape, jnp.bfloat16),
-                pltpu.SemaphoreType.DMA((req_local,)),
+                pltpu.SemaphoreType.DMA((req_local // COPIED,)),
                 pltpu.SemaphoreType.DMA,
                 pltpu.SemaphoreType.DMA,
                 pltpu.SemaphoreType.DMA,

time: 224 us -> 224 us (level)
  no operation moved by 1% of the time
where the time goes in v6:
time: 224 us; the launch traced here: 223 us
  Pallas kernels  223 us (100%)
    pallas_call x1, Pallas kernels, local_step(): pl.pallas_call(functools.partial(exchange_kernel, side), out_shape=(pltpu...  216 us
    pallas_call x1, Pallas kernels, local_step(): pl.pallas_call(functools.partial(finish_kernel, side), out_shape=(jax.Sha...  6.57 us

profile of v6, /device:TPU:97, one launch (start us, length us, event | category | flops | bytes accessed | tf_op | source)
XLA Modules:
  0.0 223.3 jit_solution(15409152443346224707)
XLA Ops:
  0.6 216.1 %exchange.1 = (bf16[16,1024,512]{2,1,0:T(8,128)(2,1)S(1)}, bf16[32,16,16,128]{3,2,1,0:T(8,128)(2,1)S(1)}, f32[16,16,128]{2,1,0:T(8,128)S(1)}, f32[16,16,128]{2,1...) custom-call(s32[1,512]{1,0:T(1,128)} %bitcast.4, ...), custom_call_target="tpu_custom_call" | custom-call | tf_op jit(solution)/shard_map/exchange/pallas_call | solution.py:364
  216.8 6.6 %finish.1 = (bf16[16,1024,512]{2,1,0:T(8,128)(2,1)}, bf16[16,64,1024]{2,1,0:T(8,128)(2,1)}, bf16[16,16,512]{2,1,0:T(8,128)(2,1)}) custom-call(bf16[16,1024,512]{2,1,0:T(8,128)(2,1)S(1)} %get-tuple-element.14.c_in, bf16[32,16,16,128]{3,2,1,0:T(8,128)(2,1)S(1)} %get-tuple-element.15.k_in, f32[16,16,128]{2,1,0:T(8,128)S(1)} %get-tuple-element.16.top, ...), custom_call_target="tpu_custom_call" | custom-call | tf_op jit(solution)/shard_map/finish/pallas_call | solution.py:400
